TPU v7x, 256 devices: a whole 4x4x8 slice. The times are simulated.
256 devices in a mesh: seq: 64 (over z, y, core), head: 4 (over x).
Axes of the slice: x: 4, y: 4, z: 8, core: 2. Of those that a mesh axis runs over, the one named last changes fastest.
Arguments:
- tail_queries: bfloat16 [10, 64, 4096], P(None, 'seq', 'head'), may hold values from -8 to 8
- keys: bfloat16 [10, 131072, 1024], P(None, 'seq', 'head'), may hold values from -160 to 160
Outputs:
- vertical: float32 [10, 32, 131072], P(None, 'head', 'seq')
- slash: float32 [10, 32, 131072], P(None, 'head', 'seq')
All inputs are finite; a program needn't handle non-finite values.
Results may differ from a plain program's by a relative error of at most 0.0003.
Values may be sent and summed in bfloat16 or wider, within the bound.
A program may use at most 64 MiB of HBM per device.

v0:
```python
import math

import jax
import jax.numpy as jnp
from jax import lax
from jax.sharding import PartitionSpec as P

HD = 128
LAST = 64


def from_everyone(shard, axis):
    copies = jnp.broadcast_to(shard, (lax.axis_size(axis), *shard.shape))
    return lax.all_to_all(copies, axis, split_axis=0, concat_axis=0, tiled=True)


def gathered_once(shard, axis):
    leaves = jax.tree.leaves(shard)
    order = sorted(range(len(leaves)), key=lambda k: -leaves[k].size)
    width = (1, *leaves[order[0]].shape)[-1]
    lines = [
        jnp.pad(leaves[k].reshape(-1), (0, -leaves[k].size % width)).reshape(-1, width)
        for k in order
    ]
    both, at, found = (from_everyone(jnp.concatenate(lines), axis), 0, {})
    for k, line in zip(order, lines):
        share = both[:, at : at + len(line)].reshape(len(both), -1)
        found[k] = share[:, : leaves[k].size].reshape(-1, *leaves[k].shape)
        at += len(line)
    numbers = iter(range(len(leaves)))
    return jax.tree.map(lambda _: found[next(numbers)], shard)


def combined_pairwise(pieces, combine):
    while len(jax.tree.leaves(pieces)[0]) > 1:
        pieces = jax.vmap(combine)(
            *(jax.tree.map(lambda part: part[side::2], pieces) for side in (0, 1))
        )
    return jax.tree.map(lambda part: part[0], pieces)


def joined_all(shard, axis, combine):
    pieces = gathered_once(shard, axis)
    return combined_pairwise(pieces, combine)


def from_behind(value, axis, steps):
    count = lax.axis_size(axis)
    initial, last = (max(0, -steps), min(count, count - steps))
    return lax.ppermute(value, axis, [(source, source + steps) for source in range(initial, last)])


def joined_along(pieces, dim):
    pieces = jnp.moveaxis(pieces, 0, dim)
    shape = pieces.shape
    return pieces.reshape(*shape[:dim], shape[dim] * shape[dim + 1], *shape[dim + 2 :])


def collect(shard, axis, dim):
    pieces = from_everyone(shard, axis)
    return joined_along(pieces, dim)


def diagonal_sums(probabilities):
    head_count, query_count, key_count = probabilities.shape
    width = key_count + (query_count + 127) // 128 * 128
    rows = jnp.pad(probabilities[:, ::-1, :], ((0, 0), (0, 0), (0, width - key_count)))
    offset = 1
    while rows.shape[1] > 1:
        even_rows = rows[:, 0::2, :]
        odd_rows = rows[:, 1::2, :]
        odd_rows = jnp.pad(odd_rows[:, :, : width - offset], ((0, 0), (0, 0), (offset, 0)))
        rows = even_rows + odd_rows
        offset = offset * 2
    return rows[:, 0, : key_count + query_count]


def merge_pair(first, second):
    larger = jnp.maximum(first[0], second[0])
    return (larger, first[1] * jnp.exp(first[0] - larger) + second[1] * jnp.exp(second[0] - larger))


def local_scores(queries, layer_keys):
    seq_count = lax.axis_size("seq")
    shard_index = lax.axis_index("seq")
    key_count = layer_keys.shape[0]
    groups = layer_keys.shape[1] // HD
    head_count = queries.shape[1] // HD
    per_group = head_count // groups
    tokens = key_count * seq_count
    grouped_queries = queries.reshape(LAST, groups, per_group, HD)
    grouped_keys = layer_keys.reshape(key_count, groups, HD)
    scores = jnp.einsum(
        "qgad,kgd->gaqk", grouped_queries, grouped_keys, preferred_element_type=jnp.float32
    )
    scores = scores.reshape(head_count, LAST, key_count) * (1.0 / math.sqrt(HD))
    positions = tokens - LAST + lax.iota(jnp.int32, LAST)
    key_positions = shard_index * key_count + lax.iota(jnp.int32, key_count)
    visible = key_positions[None, :] <= positions[:, None]
    return jnp.where(visible[None], scores, -jnp.inf)


def local_stats(scores):
    local_max = jnp.max(scores, axis=2)
    weights = jnp.exp(scores - local_max[:, :, None])
    return (local_max, weights, jnp.sum(weights, axis=2))


def spread(weights, local_max, row_max, row_total):
    factor = jnp.exp(local_max - row_max) / row_total
    probabilities = weights * factor[:, :, None]
    return (jnp.sum(probabilities, axis=1), diagonal_sums(probabilities))


def stats_each(local_max, local_total):
    return joined_all((local_max, local_total), "seq", merge_pair)


def layer_sums(queries, layer_keys):
    key_count = layer_keys.shape[0]
    ratio = key_count * lax.axis_size("seq") / LAST
    scores = local_scores(queries, layer_keys)
    local_max, weights, local_total = local_stats(scores)
    row_max, row_total = stats_each(local_max, local_total)
    vertical, skewed = spread(weights, local_max, row_max, row_total)
    overflow = from_behind(skewed[:, key_count:], "seq", 1)
    slash = skewed[:, :key_count].at[:, :LAST].add(overflow) * ratio
    return (vertical * ratio, slash)


def on_device(tail_queries, keys):
    gathered = collect(tail_queries, "seq", 1)

    def layer_step(carry, inputs):
        return (carry, layer_sums(inputs[0], inputs[1]))

    carry, results = lax.scan(layer_step, jnp.zeros((), jnp.int32), (gathered, keys))
    return (results[0], results[1])


def solution(mesh):
    return jax.shard_map(
        on_device,
        mesh=mesh,
        in_specs=(P(None, "seq", "head"), P(None, "seq", "head")),
        out_specs=(P(None, "head", "seq"), P(None, "head", "seq")),
        check_vma=False,
    )
```

profile of v0, /device:TPU:1, one launch (start us, length us, event | category | flops | bytes accessed | tf_op | source)
XLA Modules:
  0.0 618.1 jit_solution(6429434111893303315)
XLA Ops:
  3.0 13.1 %all-to-all-start.1 = ((bf16[64,10,1,1024]{3,1,2,0:T(8,128)(2,1)}), bf16[64,10,1,1024]{3,1,2,0:T(8,128)(2,1)S(1)}, u32[]{:S(2)}, u32[]{:S(2)}) async-start(bf16[64,10,1,1024]{3,1,2,0:T(8,128)(2,1)} %broadcast_in_dim.44), calls=%async_computation.1 | async-start | bytes 4194304 | tf_op jit(solution)/shard_map/all_to_all | solution.py:14
  16.2 49.7 %all-to-all-done.1 = bf16[64,10,1,1024]{3,1,2,0:T(8,128)(2,1)S(1)} async-done(((bf16[64,10,1,1024]{3,1,2,0:T(8,128)(2,1)}), bf16[64,10,1,1024]{3,1,2,0:T(8,128)(2,1)S(1)}, u32[]{:S(2)}, u32[]{:S(2)}) %all-to-all-start.1) | async-done | bytes 1310752 | tf_op jit(solution)/shard_map/all_to_all | solution.py:14
  66.6 551.5 %while.15 = (s32[]{:T(128)}, f32[10,8,2048]{2,1,0:T(8,128)}, f32[10,8,2048]{2,1,0:T(8,128)}, bf16[10,2048,256]{2,1,0:T(8,128)(2,1)}, bf16[10,64,1024]{2,1,0:T(8,...) while((s32[]{:T(128)}, f32[10,8,2048]{2,1,0:T(8,128)}, ...), condition=%wide.region_5.6_spmd, body=%wide.region_0.5_spmd.sunk | while | flops 283509312 | bytes 116966224 | solution.py:137
  81.5 12.3 %all-to-all-done = f32[64,1,1024]{2,1,0:T(1,128)S(1)} async-done(((f32[64,1,1024]{2,1,0:T(1,128)}), f32[64,1,1024]{2,1,0:T(1,128)S(1)}, u32[]{:S(2)}, u32[]{:S(2)}) %all-to-all-start) | async-done | bytes 262176 | tf_op jit(solution)/shard_map/while/body/eval_jaxpr/all_to_all | solution.py:14
  95.9 7.4 %fusion.24 = f32[8,64,2048]{2,0,1:T(8,128)} fusion(f32[8,64,2048]{2,1,0:T(8,128)} %bitcast.93, f32[8,64]{0,1:T(8,128)S(1)} %copy.49, f32[8,64]{0,1:T(8,128)S(1)} %copy.50, pred[64,2048]{1,0:T(8,128)(4,1)S(1)} %broadcast_compare_fusion.2), kind=kLoop, calls=%fused_computation.6.clone.1 | loop fusion | flops 3145728 | bytes 8523776 | tf_op jit(solution)/shard_map/while/body/eval_jaxpr/mul | solution.py:111
  127.2 8.8 %all-to-all-start = ((f32[64,1,1024]{2,1,0:T(1,128)}), f32[64,1,1024]{2,1,0:T(1,128)S(1)}, u32[]{:S(2)}, u32[]{:S(2)}) async-start(f32[64,1,1024]{2,1,0:T(1,128)} %reshape.173), calls=%async_computation | async-start | bytes 524288 | tf_op jit(solution)/shard_map/while/body/eval_jaxpr/all_to_all | solution.py:14
  136.8 12.3 %all-to-all-done = f32[64,1,1024]{2,1,0:T(1,128)S(1)} async-done(((f32[64,1,1024]{2,1,0:T(1,128)}), f32[64,1,1024]{2,1,0:T(1,128)S(1)}, u32[]{:S(2)}, u32[]{:S(2)}) %all-to-all-start) | async-done | bytes 262176 | tf_op jit(solution)/shard_map/while/body/eval_jaxpr/all_to_all | solution.py:14
  151.2 7.4 %fusion.24 = f32[8,64,2048]{2,0,1:T(8,128)} fusion(f32[8,64,2048]{2,1,0:T(8,128)} %bitcast.93, f32[8,64]{0,1:T(8,128)S(1)} %copy.49, f32[8,64]{0,1:T(8,128)S(1)} %copy.50, pred[64,2048]{1,0:T(8,128)(4,1)S(1)} %broadcast_compare_fusion.2), kind=kLoop, calls=%fused_computation.6.clone.1 | loop fusion | flops 3145728 | bytes 8523776 | tf_op jit(solution)/shard_map/while/body/eval_jaxpr/mul | solution.py:111
  182.5 8.8 %all-to-all-start = ((f32[64,1,1024]{2,1,0:T(1,128)}), f32[64,1,1024]{2,1,0:T(1,128)S(1)}, u32[]{:S(2)}, u32[]{:S(2)}) async-start(f32[64,1,1024]{2,1,0:T(1,128)} %reshape.173), calls=%async_computation | async-start | bytes 524288 | tf_op jit(solution)/shard_map/while/body/eval_jaxpr/all_to_all | solution.py:14
  192.1 12.3 %all-to-all-done = f32[64,1,1024]{2,1,0:T(1,128)S(1)} async-done(((f32[64,1,1024]{2,1,0:T(1,128)}), f32[64,1,1024]{2,1,0:T(1,128)S(1)}, u32[]{:S(2)}, u32[]{:S(2)}) %all-to-all-start) | async-done | bytes 262176 | tf_op jit(solution)/shard_map/while/body/eval_jaxpr/all_to_all | solution.py:14
  206.6 7.4 %fusion.24 = f32[8,64,2048]{2,0,1:T(8,128)} fusion(f32[8,64,2048]{2,1,0:T(8,128)} %bitcast.93, f32[8,64]{0,1:T(8,128)S(1)} %copy.49, f32[8,64]{0,1:T(8,128)S(1)} %copy.50, pred[64,2048]{1,0:T(8,128)(4,1)S(1)} %broadcast_compare_fusion.2), kind=kLoop, calls=%fused_computation.6.clone.1 | loop fusion | flops 3145728 | bytes 8523776 | tf_op jit(solution)/shard_map/while/body/eval_jaxpr/mul | solution.py:111
  237.8 8.8 %all-to-all-start = ((f32[64,1,1024]{2,1,0:T(1,128)}), f32[64,1,1024]{2,1,0:T(1,128)S(1)}, u32[]{:S(2)}, u32[]{:S(2)}) async-start(f32[64,1,1024]{2,1,0:T(1,128)} %reshape.173), calls=%async_computation | async-start | bytes 524288 | tf_op jit(solution)/shard_map/while/body/eval_jaxpr/all_to_all | solution.py:14
  247.5 12.3 %all-to-all-done = f32[64,1,1024]{2,1,0:T(1,128)S(1)} async-done(((f32[64,1,1024]{2,1,0:T(1,128)}), f32[64,1,1024]{2,1,0:T(1,128)S(1)}, u32[]{:S(2)}, u32[]{:S(2)}) %all-to-all-start) | async-done | bytes 262176 | tf_op jit(solution)/shard_map/while/body/eval_jaxpr/all_to_all | solution.py:14
  261.9 7.4 %fusion.24 = f32[8,64,2048]{2,0,1:T(8,128)} fusion(f32[8,64,2048]{2,1,0:T(8,128)} %bitcast.93, f32[8,64]{0,1:T(8,128)S(1)} %copy.49, f32[8,64]{0,1:T(8,128)S(1)} %copy.50, pred[64,2048]{1,0:T(8,128)(4,1)S(1)} %broadcast_compare_fusion.2), kind=kLoop, calls=%fused_computation.6.clone.1 | loop fusion | flops 3145728 | bytes 8523776 | tf_op jit(solution)/shard_map/while/body/eval_jaxpr/mul | solution.py:111
  293.2 8.8 %all-to-all-start = ((f32[64,1,1024]{2,1,0:T(1,128)}), f32[64,1,1024]{2,1,0:T(1,128)S(1)}, u32[]{:S(2)}, u32[]{:S(2)}) async-start(f32[64,1,1024]{2,1,0:T(1,128)} %reshape.173), calls=%async_computation | async-start | bytes 524288 | tf_op jit(solution)/shard_map/while/body/eval_jaxpr/all_to_all | solution.py:14
  302.8 12.3 %all-to-all-done = f32[64,1,1024]{2,1,0:T(1,128)S(1)} async-done(((f32[64,1,1024]{2,1,0:T(1,128)}), f32[64,1,1024]{2,1,0:T(1,128)S(1)}, u32[]{:S(2)}, u32[]{:S(2)}) %all-to-all-start) | async-done | bytes 262176 | tf_op jit(solution)/shard_map/while/body/eval_jaxpr/all_to_all | solution.py:14
  317.2 7.4 %fusion.24 = f32[8,64,2048]{2,0,1:T(8,128)} fusion(f32[8,64,2048]{2,1,0:T(8,128)} %bitcast.93, f32[8,64]{0,1:T(8,128)S(1)} %copy.49, f32[8,64]{0,1:T(8,128)S(1)} %copy.50, pred[64,2048]{1,0:T(8,128)(4,1)S(1)} %broadcast_compare_fusion.2), kind=kLoop, calls=%fused_computation.6.clone.1 | loop fusion | flops 3145728 | bytes 8523776 | tf_op jit(solution)/shard_map/while/body/eval_jaxpr/mul | solution.py:111
  348.5 8.8 %all-to-all-start = ((f32[64,1,1024]{2,1,0:T(1,128)}), f32[64,1,1024]{2,1,0:T(1,128)S(1)}, u32[]{:S(2)}, u32[]{:S(2)}) async-start(f32[64,1,1024]{2,1,0:T(1,128)} %reshape.173), calls=%async_computation | async-start | bytes 524288 | tf_op jit(solution)/shard_map/while/body/eval_jaxpr/all_to_all | solution.py:14
  358.1 12.3 %all-to-all-done = f32[64,1,1024]{2,1,0:T(1,128)S(1)} async-done(((f32[64,1,1024]{2,1,0:T(1,128)}), f32[64,1,1024]{2,1,0:T(1,128)S(1)}, u32[]{:S(2)}, u32[]{:S(2)}) %all-to-all-start) | async-done | bytes 262176 | tf_op jit(solution)/shard_map/while/body/eval_jaxpr/all_to_all | solution.py:14
  372.6 7.4 %fusion.24 = f32[8,64,2048]{2,0,1:T(8,128)} fusion(f32[8,64,2048]{2,1,0:T(8,128)} %bitcast.93, f32[8,64]{0,1:T(8,128)S(1)} %copy.49, f32[8,64]{0,1:T(8,128)S(1)} %copy.50, pred[64,2048]{1,0:T(8,128)(4,1)S(1)} %broadcast_compare_fusion.2), kind=kLoop, calls=%fused_computation.6.clone.1 | loop fusion | flops 3145728 | bytes 8523776 | tf_op jit(solution)/shard_map/while/body/eval_jaxpr/mul | solution.py:111
  403.8 8.8 %all-to-all-start = ((f32[64,1,1024]{2,1,0:T(1,128)}), f32[64,1,1024]{2,1,0:T(1,128)S(1)}, u32[]{:S(2)}, u32[]{:S(2)}) async-start(f32[64,1,1024]{2,1,0:T(1,128)} %reshape.173), calls=%async_computation | async-start | bytes 524288 | tf_op jit(solution)/shard_map/while/body/eval_jaxpr/all_to_all | solution.py:14
  413.5 12.3 %all-to-all-done = f32[64,1,1024]{2,1,0:T(1,128)S(1)} async-done(((f32[64,1,1024]{2,1,0:T(1,128)}), f32[64,1,1024]{2,1,0:T(1,128)S(1)}, u32[]{:S(2)}, u32[]{:S(2)}) %all-to-all-start) | async-done | bytes 262176 | tf_op jit(solution)/shard_map/while/body/eval_jaxpr/all_to_all | solution.py:14
  427.9 7.4 %fusion.24 = f32[8,64,2048]{2,0,1:T(8,128)} fusion(f32[8,64,2048]{2,1,0:T(8,128)} %bitcast.93, f32[8,64]{0,1:T(8,128)S(1)} %copy.49, f32[8,64]{0,1:T(8,128)S(1)} %copy.50, pred[64,2048]{1,0:T(8,128)(4,1)S(1)} %broadcast_compare_fusion.2), kind=kLoop, calls=%fused_computation.6.clone.1 | loop fusion | flops 3145728 | bytes 8523776 | tf_op jit(solution)/shard_map/while/body/eval_jaxpr/mul | solution.py:111
  459.2 8.8 %all-to-all-start = ((f32[64,1,1024]{2,1,0:T(1,128)}), f32[64,1,1024]{2,1,0:T(1,128)S(1)}, u32[]{:S(2)}, u32[]{:S(2)}) async-start(f32[64,1,1024]{2,1,0:T(1,128)} %reshape.173), calls=%async_computation | async-start | bytes 524288 | tf_op jit(solution)/shard_map/while/body/eval_jaxpr/all_to_all | solution.py:14
  468.8 12.3 %all-to-all-done = f32[64,1,1024]{2,1,0:T(1,128)S(1)} async-done(((f32[64,1,1024]{2,1,0:T(1,128)}), f32[64,1,1024]{2,1,0:T(1,128)S(1)}, u32[]{:S(2)}, u32[]{:S(2)}) %all-to-all-start) | async-done | bytes 262176 | tf_op jit(solution)/shard_map/while/body/eval_jaxpr/all_to_all | solution.py:14
  483.2 7.4 %fusion.24 = f32[8,64,2048]{2,0,1:T(8,128)} fusion(f32[8,64,2048]{2,1,0:T(8,128)} %bitcast.93, f32[8,64]{0,1:T(8,128)S(1)} %copy.49, f32[8,64]{0,1:T(8,128)S(1)} %copy.50, pred[64,2048]{1,0:T(8,128)(4,1)S(1)} %broadcast_compare_fusion.2), kind=kLoop, calls=%fused_computation.6.clone.1 | loop fusion | flops 3145728 | bytes 8523776 | tf_op jit(solution)/shard_map/while/body/eval_jaxpr/mul | solution.py:111
  514.5 8.8 %all-to-all-start = ((f32[64,1,1024]{2,1,0:T(1,128)}), f32[64,1,1024]{2,1,0:T(1,128)S(1)}, u32[]{:S(2)}, u32[]{:S(2)}) async-start(f32[64,1,1024]{2,1,0:T(1,128)} %reshape.173), calls=%async_computation | async-start | bytes 524288 | tf_op jit(solution)/shard_map/while/body/eval_jaxpr/all_to_all | solution.py:14
  524.2 12.3 %all-to-all-done = f32[64,1,1024]{2,1,0:T(1,128)S(1)} async-done(((f32[64,1,1024]{2,1,0:T(1,128)}), f32[64,1,1024]{2,1,0:T(1,128)S(1)}, u32[]{:S(2)}, u32[]{:S(2)}) %all-to-all-start) | async-done | bytes 262176 | tf_op jit(solution)/shard_map/while/body/eval_jaxpr/all_to_all | solution.py:14
  538.6 7.4 %fusion.24 = f32[8,64,2048]{2,0,1:T(8,128)} fusion(f32[8,64,2048]{2,1,0:T(8,128)} %bitcast.93, f32[8,64]{0,1:T(8,128)S(1)} %copy.49, f32[8,64]{0,1:T(8,128)S(1)} %copy.50, pred[64,2048]{1,0:T(8,128)(4,1)S(1)} %broadcast_compare_fusion.2), kind=kLoop, calls=%fused_computation.6.clone.1 | loop fusion | flops 3145728 | bytes 8523776 | tf_op jit(solution)/shard_map/while/body/eval_jaxpr/mul | solution.py:111
  569.8 8.8 %all-to-all-start = ((f32[64,1,1024]{2,1,0:T(1,128)}), f32[64,1,1024]{2,1,0:T(1,128)S(1)}, u32[]{:S(2)}, u32[]{:S(2)}) async-start(f32[64,1,1024]{2,1,0:T(1,128)} %reshape.173), calls=%async_computation | async-start | bytes 524288 | tf_op jit(solution)/shard_map/while/body/eval_jaxpr/all_to_all | solution.py:14
  579.5 12.3 %all-to-all-done = f32[64,1,1024]{2,1,0:T(1,128)S(1)} async-done(((f32[64,1,1024]{2,1,0:T(1,128)}), f32[64,1,1024]{2,1,0:T(1,128)S(1)}, u32[]{:S(2)}, u32[]{:S(2)}) %all-to-all-start) | async-done | bytes 262176 | tf_op jit(solution)/shard_map/while/body/eval_jaxpr/all_to_all | solution.py:14
  593.9 7.4 %fusion.24 = f32[8,64,2048]{2,0,1:T(8,128)} fusion(f32[8,64,2048]{2,1,0:T(8,128)} %bitcast.93, f32[8,64]{0,1:T(8,128)S(1)} %copy.49, f32[8,64]{0,1:T(8,128)S(1)} %copy.50, pred[64,2048]{1,0:T(8,128)(4,1)S(1)} %broadcast_compare_fusion.2), kind=kLoop, calls=%fused_computation.6.clone.1 | loop fusion | flops 3145728 | bytes 8523776 | tf_op jit(solution)/shard_map/while/body/eval_jaxpr/mul | solution.py:111
  (575 shorter events, 275.4 us)
Async XLA Ops:
  3.0 62.9 %all-to-all-start.1 = ((bf16[64,10,1,1024]{3,1,2,0:T(8,128)(2,1)}), bf16[64,10,1,1024]{3,1,2,0:T(8,128)(2,1)S(1)}, u32[]{:S(2)}, u32[]{:S(2)}) async-start(bf16[64,10,1,1024]{3,1,2,0:T(8,128)(2,1)} %broadcast_in_dim.44), calls=%async_computation.1 | async-start | bytes 4194304 | tf_op jit(solution)/shard_map/all_to_all | solution.py:14
  73.7 20.0 %all-to-all-start = ((f32[64,1,1024]{2,1,0:T(1,128)}), f32[64,1,1024]{2,1,0:T(1,128)S(1)}, u32[]{:S(2)}, u32[]{:S(2)}) async-start(f32[64,1,1024]{2,1,0:T(1,128)} %reshape.173), calls=%async_computation | async-start | bytes 524288 | tf_op jit(solution)/shard_map/while/body/eval_jaxpr/all_to_all | solution.py:14
  107.9 2.8 copy-start.2
  111.5 2.2 copy-start.1
  115.1 3.4 collective-permute-start
  127.2 21.9 %all-to-all-start = ((f32[64,1,1024]{2,1,0:T(1,128)}), f32[64,1,1024]{2,1,0:T(1,128)S(1)}, u32[]{:S(2)}, u32[]{:S(2)}) async-start(f32[64,1,1024]{2,1,0:T(1,128)} %reshape.173), calls=%async_computation | async-start | bytes 524288 | tf_op jit(solution)/shard_map/while/body/eval_jaxpr/all_to_all | solution.py:14
  163.3 2.8 copy-start.2
  170.4 3.4 collective-permute-start
  182.5 21.9 %all-to-all-start = ((f32[64,1,1024]{2,1,0:T(1,128)}), f32[64,1,1024]{2,1,0:T(1,128)S(1)}, u32[]{:S(2)}, u32[]{:S(2)}) async-start(f32[64,1,1024]{2,1,0:T(1,128)} %reshape.173), calls=%async_computation | async-start | bytes 524288 | tf_op jit(solution)/shard_map/while/body/eval_jaxpr/all_to_all | solution.py:14
  218.6 2.8 copy-start.2
  225.7 3.4 collective-permute-start
  237.8 21.9 %all-to-all-start = ((f32[64,1,1024]{2,1,0:T(1,128)}), f32[64,1,1024]{2,1,0:T(1,128)S(1)}, u32[]{:S(2)}, u32[]{:S(2)}) async-start(f32[64,1,1024]{2,1,0:T(1,128)} %reshape.173), calls=%async_computation | async-start | bytes 524288 | tf_op jit(solution)/shard_map/while/body/eval_jaxpr/all_to_all | solution.py:14
  274.0 2.8 copy-start.2
  281.1 3.4 collective-permute-start
  293.2 21.9 %all-to-all-start = ((f32[64,1,1024]{2,1,0:T(1,128)}), f32[64,1,1024]{2,1,0:T(1,128)S(1)}, u32[]{:S(2)}, u32[]{:S(2)}) async-start(f32[64,1,1024]{2,1,0:T(1,128)} %reshape.173), calls=%async_computation | async-start | bytes 524288 | tf_op jit(solution)/shard_map/while/body/eval_jaxpr/all_to_all | solution.py:14
  329.3 2.8 copy-start.2
  336.4 3.4 collective-permute-start
  348.5 21.9 %all-to-all-start = ((f32[64,1,1024]{2,1,0:T(1,128)}), f32[64,1,1024]{2,1,0:T(1,128)S(1)}, u32[]{:S(2)}, u32[]{:S(2)}) async-start(f32[64,1,1024]{2,1,0:T(1,128)} %reshape.173), calls=%async_computation | async-start | bytes 524288 | tf_op jit(solution)/shard_map/while/body/eval_jaxpr/all_to_all | solution.py:14
  384.6 2.8 copy-start.2
  391.7 3.4 collective-permute-start
  403.8 21.9 %all-to-all-start = ((f32[64,1,1024]{2,1,0:T(1,128)}), f32[64,1,1024]{2,1,0:T(1,128)S(1)}, u32[]{:S(2)}, u32[]{:S(2)}) async-start(f32[64,1,1024]{2,1,0:T(1,128)} %reshape.173), calls=%async_computation | async-start | bytes 524288 | tf_op jit(solution)/shard_map/while/body/eval_jaxpr/all_to_all | solution.py:14
  440.0 2.8 copy-start.2
  447.1 3.4 collective-permute-start
  459.2 21.9 %all-to-all-start = ((f32[64,1,1024]{2,1,0:T(1,128)}), f32[64,1,1024]{2,1,0:T(1,128)S(1)}, u32[]{:S(2)}, u32[]{:S(2)}) async-start(f32[64,1,1024]{2,1,0:T(1,128)} %reshape.173), calls=%async_computation | async-start | bytes 524288 | tf_op jit(solution)/shard_map/while/body/eval_jaxpr/all_to_all | solution.py:14
  495.3 2.8 copy-start.2
  502.4 3.4 collective-permute-start
  514.5 21.9 %all-to-all-start = ((f32[64,1,1024]{2,1,0:T(1,128)}), f32[64,1,1024]{2,1,0:T(1,128)S(1)}, u32[]{:S(2)}, u32[]{:S(2)}) async-start(f32[64,1,1024]{2,1,0:T(1,128)} %reshape.173), calls=%async_computation | async-start | bytes 524288 | tf_op jit(solution)/shard_map/while/body/eval_jaxpr/all_to_all | solution.py:14
  550.6 2.8 copy-start.2
  557.7 3.4 collective-permute-start
  569.8 21.9 %all-to-all-start = ((f32[64,1,1024]{2,1,0:T(1,128)}), f32[64,1,1024]{2,1,0:T(1,128)S(1)}, u32[]{:S(2)}, u32[]{:S(2)}) async-start(f32[64,1,1024]{2,1,0:T(1,128)} %reshape.173), calls=%async_computation | async-start | bytes 524288 | tf_op jit(solution)/shard_map/while/body/eval_jaxpr/all_to_all | solution.py:14
  606.0 2.8 copy-start.2
  613.1 3.4 collective-permute-start
  (19 other events, 39.1 us)
where the time goes:
time: 622 us; the launch traced here: 618 us
  waiting for transfers between devices  173 us (28%)
  local copies, waits for them, and re-layouts  159 us (26%)
  other arithmetic  147 us (24%)
  starting transfers between devices  126 us (20%)
  matrix products  8.92 us (1%)
    all_to_all x11, waiting for transfers between devices, from_everyone(): return lax.all_to_all(copies, axis, split_axis=0, concat_axis=0, tiled=True)  172 us
    all_to_all x11, starting transfers between devices, from_everyone(): return lax.all_to_all(copies, axis, split_axis=0, concat_axis=0, tiled=True)  99.7 us
    mul x10, other arithmetic, spread(): probabilities = weights * factor[:, :, None]  74.1 us
    while x80, local copies, waits for them, and re-layouts  52.1 us
    rev x10, local copies, waits for them, and re-layouts, diagonal_sums(): probabilities[:, ::-1, :]  46.4 us
    ppermute x10, starting transfers between devices, from_behind(): lax.ppermute(value, axis, [(source, source + steps) for source in range(i...  26.6 us
    slice x50, local copies, waits for them, and re-layouts, diagonal_sums(): odd_rows = rows[:, 1::2, :]  20.4 us
    dynamic_slice x30, local copies, waits for them, and re-layouts, on_device(): lax.scan(layer_step, jnp.zeros((), jnp.int32), (gathered, keys))  19.6 us
  transfers between devices with their start and end apart: 21, of which 21 were waited for; matrix products, arithmetic and copies ran while one was open for 2% of the time, Pallas kernels for 0%

commit v1 on v0

v1 whole, which is shorter than its diff:
```python
import functools
import math

import jax
import jax.numpy as jnp
from jax import lax
from jax.experimental import pallas as pl
from jax.experimental.pallas import tpu as pltpu
from jax.sharding import PartitionSpec as P

HD = 128
LAST = 64
LANES = 128
F32 = jnp.float32
BF16 = jnp.bfloat16
SCALE = math.log2(math.e) / math.sqrt(HD)
CHUNK = 2
NZ, NY, NC = 8, 4, 2
NR = NY * NC


def tree(op, xs):
    xs = list(xs)
    while len(xs) > 1:
        xs = [op(*xs[n : n + 2]) if n + 1 < len(xs) else xs[n] for n in range(0, len(xs), 2)]
    return xs[0]


def combined(parts):
    top = tree(jnp.maximum, parts)
    return top + jnp.log2(tree(jnp.add, [jnp.exp2(part - top) for part in parts]))


def score(q, k_ref, layer, group, s_ref):
    keys = s_ref.shape[1]
    for n in range(0, keys, 256):
        k = k_ref[layer, n : n + 256, HD * group : HD * group + HD]
        s_ref[:, n : n + 256] = lax.dot_general(
            q, k, (((1,), (1,)), ((), ())), preferred_element_type=F32
        )


def weigh(s_ref, w_ref, m_ref, t_ref, limit):
    rows, keys = s_ref.shape
    lane = lax.broadcasted_iota(jnp.int32, (8, LANES), 1)
    sub = lax.broadcasted_iota(jnp.int32, (8, LANES), 0)
    ahead = lane - jnp.where(sub >= 4, 1, 0)
    for v in range(rows // 8):
        at = slice(8 * v, 8 * v + 8)
        xs = [s_ref[at, n : n + LANES] for n in range(0, keys, LANES)]
        xs[-1] = jnp.where(ahead > limit + 2 * v, -jnp.inf, xs[-1])
        top = tree(jnp.maximum, xs)
        ws = [jnp.exp2((x - top) * SCALE) for x in xs]
        for n, w in enumerate(ws):
            w_ref[at, n * LANES : n * LANES + LANES] = w
        m_ref[at, :] = top
        t_ref[at, :] = tree(jnp.add, ws)


def row_stats(m_ref, t_ref, mt_ref):
    mt = m_ref[...].T
    mt_ref[...] = mt
    top = jnp.max(mt, axis=0, keepdims=True)
    total = jnp.sum(t_ref[...].T * jnp.exp2((mt - top) * SCALE), axis=0, keepdims=True)
    return top * SCALE + jnp.log2(total)


def spread(w_ref, f_ref, vert_ref, slash_ref, over_ref, group):
    rows, keys = w_ref.shape
    tiles = keys // LANES
    lane = lax.broadcasted_iota(jnp.int32, (8, LANES), 1)
    zero = jnp.zeros((8, LANES), F32)
    vert = [zero] * tiles
    slash = [zero] * (tiles + 1)
    for v in range(rows // 8):
        at = slice(8 * v, 8 * v + 8)
        shift = LAST - 2 - 2 * v
        factor = f_ref[at, :]
        wrapped = lane < shift
        before = zero
        for n in range(tiles):
            p = w_ref[at, n * LANES : n * LANES + LANES] * factor
            vert[n] = vert[n] + p
            if shift:
                turned = pltpu.roll(p, shift, 1)
                p = jnp.where(wrapped, before, turned)
                before = turned
            slash[n] = slash[n] + p
        if shift:
            slash[tiles] = slash[tiles] + jnp.where(wrapped, before, 0.0)
    before = zero
    heads = slice(4 * group, 4 * group + 4)
    for n in range(tiles + 1):
        turned = pltpu.roll(slash[n], 1, 1)
        y = jnp.where(lane < 1, before, turned)[0:4] + slash[n][4:8]
        before = turned
        if n < tiles:
            slash_ref[heads, n * LANES : n * LANES + LANES] = y
            vert_ref[heads, n * LANES : n * LANES + LANES] = vert[n][0:4] + vert[n][4:8]
        else:
            over_ref[heads, :] = y


def kernel(
    q_hbm, k_hbm, vert_hbm, slash_hbm,
    qg, kv, sa, sb, wv, mv, tv, mt, fv, vo, so, over, over_in, st1, st2, total,
    q_sem, k_sem, o_sem,
    z_send, z_recv, y_send, y_recv, c_send, c_recv,
    s1_send, s1_recv, s2_send, s2_recv, d_send, d_recv,
):
    layers = kv.shape[0]
    chunks = layers // CHUNK
    seq = lax.axis_index("seq")
    z, r = seq // NR, lax.rem(seq, NR)
    y, c = r // NC, lax.rem(r, NC)
    z_peer = lambda n: lax.rem(z + n, NZ) * NR + r
    r_peer = lambda n: z * NR + lax.rem(r + n, NR)
    ahead, behind = lax.rem(seq + 1, NZ * NR), lax.rem(seq + NZ * NR - 1, NZ * NR)
    count = lax.axis_size("seq")
    limit = LAST + jnp.where(seq == count - 1, 0, 1000)

    own = pltpu.make_async_copy(q_hbm, qg.at[z, y, c], q_sem)
    own.start()
    key_copy = lambda n: pltpu.make_async_copy(k_hbm.at[n], kv.at[n], k_sem.at[n])
    for n in range(layers):
        key_copy(n).start()

    barrier = pltpu.get_barrier_semaphore()
    greeted = [z_peer(n) for n in range(1, NZ)] + [r_peer(n) for n in range(1, NR)] + [ahead, behind]
    for peer in greeted:
        pl.semaphore_signal(barrier, inc=1, device_id={"seq": peer}, device_id_type=pl.DeviceIdType.MESH)

    def remote(src, dst, send, recv, peer):
        return pltpu.make_async_remote_copy(
            src_ref=src, dst_ref=dst, send_sem=send, recv_sem=recv,
            device_id={"seq": peer}, device_id_type=pl.DeviceIdType.MESH,
        )

    part = lambda k: pl.ds(CHUNK * k, CHUNK)

    def z_copy(k, n, zz):
        block = qg.at[zz, y, c, part(k)]
        return remote(block, block, z_send.at[k, n - 1], z_recv.at[k, n - 1], z_peer(n))

    def y_copy(k, n, yy):
        block = qg.at[:, yy, c, part(k)]
        peer = z * NR + lax.rem(y + n, NY) * NC + c
        return remote(block, block, y_send.at[k, n - 1], y_recv.at[k, n - 1], peer)

    def c_copy(k, cc):
        block = qg.at[:, :, cc, part(k)]
        return remote(block, block, c_send.at[k], c_recv.at[k], z * NR + y * NC + 1 - c)

    def s1_copy(k, n, zz):
        block = st1.at[k, zz]
        return remote(block, block, s1_send.at[k, n - 1], s1_recv.at[k, n - 1], z_peer(n))

    def s2_copy(k, n, rr):
        block = st2.at[k, rr]
        return remote(block, block, s2_send.at[k, n - 1], s2_recv.at[k, n - 1], r_peer(n))

    def d_copy(k):
        return remote(over.at[part(k)], over_in.at[part(k)], d_send.at[k], d_recv.at[k], ahead)

    def z_to_y(k):
        for n in range(1, NZ):
            z_copy(k, n, lax.rem(z + NZ - n, NZ)).wait_recv()
        for n in range(1, NY):
            y_copy(k, n, y).start()

    def y_to_c(k):
        for n in range(1, NY):
            y_copy(k, n, lax.rem(y + NY - n, NY)).wait_recv()
        c_copy(k, c).start()

    def s1_to_s2(k):
        for n in range(1, NZ):
            s1_copy(k, n, lax.rem(z + NZ - n, NZ)).wait_recv()
        st2[k, r] = combined([st1[k, n] for n in range(NZ)])
        for n in range(1, NR):
            s2_copy(k, n, r).start()

    def queries(layer, group):
        return qg[:, :, :, layer, group].reshape(-1, HD)

    own.wait()
    pl.semaphore_wait(barrier, len(greeted))
    for k in range(chunks):
        for n in range(1, NZ):
            z_copy(k, n, z).start()
    z_to_y(0)
    z_to_y(1)
    y_to_c(0)
    key_copy(0).wait()
    c_copy(0, 1 - c).wait_recv()
    score(queries(0, 0), kv, 0, 0, sa)

    def gather_stats(k, row, m_ref, t_ref, mt_ref):
        found = row_stats(m_ref, t_ref, mt_ref)
        for half in range(2):
            st1[k, z, pl.ds(2 * row + half, 1), :] = found[:, half * LANES : half * LANES + LANES]

    def first_pass(k, carry):
        @pl.when(k + 1 < chunks)
        def _():
            y_to_c(k + 1)

        @pl.when(k + 2 < chunks)
        def _():
            z_to_y(k + 2)

        def layer_pass(j, carry):
            layer = CHUNK * k + j
            following = jnp.minimum(layer + 1, layers - 1)
            score(queries(layer, 1), kv, layer, 1, sb)
            weigh(sa, wv.at[layer, 0], mv.at[0], tv.at[0], limit)
            gather_stats(k, 2 * j, mv.at[0], tv.at[0], mt.at[layer, 0])

            @pl.when(layer + 1 < layers)
            def _():
                key_copy(layer + 1).wait()

            @pl.when((j == CHUNK - 1) & (k + 1 < chunks))
            def _():
                c_copy(k + 1, 1 - c).wait_recv()

            score(queries(following, 0), kv, following, 0, sa)
            weigh(sb, wv.at[layer, 1], mv.at[1], tv.at[1], limit)
            gather_stats(k, 2 * j + 1, mv.at[1], tv.at[1], mt.at[layer, 1])
            return carry

        lax.fori_loop(0, CHUNK, layer_pass, 0)
        for n in range(1, NZ):
            s1_copy(k, n, z).start()

        @pl.when(k > 0)
        def _():
            s1_to_s2(k - 1)

        return carry

    lax.fori_loop(0, chunks, first_pass, 0)

    def out_copies(k):
        return [
            pltpu.make_async_copy(vo.at[part(k)], vert_hbm.at[part(k)], o_sem.at[k, 0]),
            pltpu.make_async_copy(so.at[part(k)], slash_hbm.at[part(k)], o_sem.at[k, 1]),
        ]

    def finish(k):
        d_copy(k).wait_recv()
        for j in range(CHUNK):
            so[CHUNK * k + j, :, 0:LANES] = so[CHUNK * k + j, :, 0:LANES] + over_in[CHUNK * k + j]
        for copy in out_copies(k):
            copy.start()

    def second_pass(k, carry):
        for n in range(1, NR):
            s2_copy(k, n, lax.rem(r + NR - n, NR)).wait_recv()
        total[...] = math.log2(so.shape[2] * count / LAST) - combined([st2[k, n] for n in range(NR)])

        def layer_pass(j, carry):
            layer = CHUNK * k + j
            for group in range(2):
                for half in range(2):
                    at = slice(half * LANES, half * LANES + LANES)
                    offset = total[pl.ds(4 * j + 2 * group + half, 1), :]
                    fv[group, at, :] = jnp.exp2(mt[layer, group, :, at] * SCALE + offset).T
                spread(
                    wv.at[layer, group], fv.at[group],
                    vo.at[layer], so.at[layer], over.at[layer], group,
                )
            return carry

        lax.fori_loop(0, CHUNK, layer_pass, 0)
        d_copy(k).start()

        @pl.when(k == 0)
        def _():
            s1_to_s2(chunks - 1)

        @pl.when(k > 0)
        def _():
            finish(k - 1)

        return carry

    lax.fori_loop(0, chunks, second_pass, 0)
    finish(chunks - 1)

    def drain(k, carry):
        for n in range(1, NZ):
            z_copy(k, n, z).wait_send()
            s1_copy(k, n, z).wait_send()
        for n in range(1, NY):
            y_copy(k, n, y).wait_send()
        for n in range(1, NR):
            s2_copy(k, n, r).wait_send()
        c_copy(k, c).wait_send()
        d_copy(k).wait_send()
        for copy in out_copies(k):
            copy.wait()
        return carry

    lax.fori_loop(0, chunks, drain, 0)


def on_device(tail_queries, keys):
    layers, key_count, width = keys.shape
    groups = width // HD
    heads = tail_queries.shape[2] // HD
    per_group = heads // groups
    rows = LAST * per_group
    chunks = layers // CHUNK
    q = tail_queries.reshape(layers, groups, per_group, HD)
    out = jax.ShapeDtypeStruct((layers, heads, key_count), F32)
    dma = pltpu.SemaphoreType.DMA
    return pl.pallas_call(
        kernel,
        out_shape=(out, out),
        in_specs=[pl.BlockSpec(memory_space=pl.ANY)] * 2,
        out_specs=[pl.BlockSpec(memory_space=pl.ANY)] * 2,
        scratch_shapes=[
            pltpu.VMEM((NZ, NY, NC, layers, groups, per_group, HD), BF16),
            pltpu.VMEM((layers, key_count, width), BF16),
            pltpu.VMEM((rows, key_count), F32),
            pltpu.VMEM((rows, key_count), F32),
            pltpu.VMEM((layers, groups, rows, key_count), F32),
            pltpu.VMEM((groups, rows, LANES), F32),
            pltpu.VMEM((groups, rows, LANES), F32),
            pltpu.VMEM((layers, groups, LANES, rows), F32),
            pltpu.VMEM((groups, rows, LANES), F32),
            pltpu.VMEM((layers, heads, key_count), F32),
            pltpu.VMEM((layers, heads, key_count), F32),
            pltpu.VMEM((layers, heads, LANES), F32),
            pltpu.VMEM((layers, heads, LANES), F32),
            pltpu.VMEM((chunks, NZ, 8, LANES), F32),
            pltpu.VMEM((chunks, NR, 8, LANES), F32),
            pltpu.VMEM((8, LANES), F32),
            dma,
            dma((layers,)),
            dma((chunks, 2)),
            dma((chunks, NZ - 1)),
            dma((chunks, NZ - 1)),
            dma((chunks, NY - 1)),
            dma((chunks, NY - 1)),
            dma((chunks,)),
            dma((chunks,)),
            dma((chunks, NZ - 1)),
            dma((chunks, NZ - 1)),
            dma((chunks, NR - 1)),
            dma((chunks, NR - 1)),
            dma((chunks,)),
            dma((chunks,)),
        ],
        compiler_params=pltpu.CompilerParams(
            collective_id=0, has_side_effects=True, vmem_limit_bytes=67043328
        ),
    )(q, keys)


def solution(mesh):
    return jax.shard_map(
        on_device,
        mesh=mesh,
        in_specs=(P(None, "seq", "head"), P(None, "seq", "head")),
        out_specs=(P(None, "head", "seq"), P(None, "head", "seq")),
        check_vma=False,
    )
```

time: 622 us -> 66.1 us (0.11)
  waiting for transfers between devices: 173 us -> 0 us
  local copies, waits for them, and re-layouts: 159 us -> 5.33 us
  other arithmetic: 147 us -> 0 us
  starting transfers between devices: 126 us -> 0 us
  Pallas kernels: 0 us -> 59.9 us
  matrix products: 8.92 us -> 0 us
    all_to_all x11 -> x0, waiting for transfers between devices: 172 us -> none  [from_everyone(): return lax.all_to_all(copies, axis, split_axis=0, concat_axis=0, tiled=True)]
    all_to_all x11 -> x0, starting transfers between devices: 99.7 us -> none  [from_everyone(): return lax.all_to_all(copies, axis, split_axis=0, concat_axis=0, tiled=True)]
    mul x20 -> x0, other arithmetic: 74.3 us -> none  [the longest x10 74.1 us: spread(): probabilities = weights * factor[:, :, None]]
    pallas_call x0 -> x1, Pallas kernels: none -> 59.9 us  [on_device(): pl.pallas_call(kernel, out_shape=(out, out), in_specs=[pl.BlockSpec(memor...]
    while x81 -> x0, local copies, waits for them, and re-layouts: 52.8 us -> none
    rev x10 -> x0, local copies, waits for them, and re-layouts: 46.4 us -> none  [diagonal_sums(): probabilities[:, ::-1, :]]
    ppermute x10 -> x0, starting transfers between devices: 26.6 us -> none  [from_behind(): lax.ppermute(value, axis, [(source, source + steps) for source in range(i...]
    reduce_sum x20 -> x0, other arithmetic: 22 us -> none  [the longest x10 12.1 us: spread(): return (jnp.sum(probabilities, axis=1), diagonal_sums(probabilities))]
  transfers between devices with their start and end apart: 21 -> 0, of which waited for: 21 -> 0; matrix products, arithmetic and copies ran while one was open for 2% -> 0% of each run, Pallas kernels for 0% -> 0%
where the time goes in v1:
time: 66.1 us; the launch traced here: 65.9 us
  Pallas kernels  59.9 us (91%)
  local copies, waits for them, and re-layouts  5.33 us (8%)
    pallas_call x1, Pallas kernels, on_device(): pl.pallas_call(kernel, out_shape=(out, out), in_specs=[pl.BlockSpec(memor...  59.9 us
    unnamed x2, local copies, waits for them, and re-layouts  3.95 us
    reshape x1, local copies, waits for them, and re-layouts, on_device(): q = tail_queries.reshape(layers, groups, per_group, HD)  1.38 us

profile of v1, /device:TPU:1, one launch (start us, length us, event | category | flops | bytes accessed | tf_op | source)
XLA Modules:
  0.0 65.9 jit_solution(1558039731963234509)
XLA Ops:
  0.6 1.4 %reshape.7.q_hbm = bf16[10,2,4,128]{3,2,1,0:T(4,128)(2,1)} reshape(bf16[10,1,1024]{2,0,1:T(8,128)(2,1)} %param.2) | data formatting | bytes 40960 | tf_op jit(solution)/shard_map/reshape | solution.py:315
  2.0 59.9 %shard_map.41 = (f32[10,8,2048]{2,1,0:T(8,128)}, f32[10,8,2048]{2,1,0:T(8,128)}) custom-call(bf16[10,2,4,128]{3,2,1,0:T(4,128)(2,1)} %reshape.7.q_hbm, bf16[10,2048,256]{2,1,0:T(8,128)(2,1)} %k_hbm.1), custom_call_target="tpu_custom_call" | custom-call | tf_op jit(solution)/shard_map/pallas_call | solution.py:318
  61.9 2.0 %copy.6 = f32[10,8,2048]{2,1,0:T(8,128)} copy(f32[10,8,2048]{2,1,0:T(8,128)} %get-tuple-element.4) | data formatting | bytes 1310720
  63.9 2.0 %copy.7 = f32[10,8,2048]{2,1,0:T(8,128)} copy(f32[10,8,2048]{2,1,0:T(8,128)} %get-tuple-element.5) | data formatting | bytes 1310720

commit v2 on v1

--- a/solution.py
+++ b/solution.py
@@ -17,6 +17,9 @@
 CHUNK = 2
 NZ, NY, NC = 8, 4, 2
 NR = NY * NC
+TILES = 16
+TAUS = TILES + LAST // 2 - 1
+BIASES = 2 * TILES
 
 
 def tree(op, xs):
@@ -32,23 +35,33 @@
 
 
 def score(q, k_ref, layer, group, s_ref):
-    keys = s_ref.shape[1]
-    for n in range(0, keys, 256):
-        k = k_ref[layer, n : n + 256, HD * group : HD * group + HD]
-        s_ref[:, n : n + 256] = lax.dot_general(
+    for n in range(0, TILES, 2):
+        tile = lambda m: k_ref[layer, m % 4, :, m // 4, :, HD * group : HD * group + HD].reshape(LANES, HD)
+        k = jnp.concatenate([tile(n), tile(n + 1)], axis=0)
+        s_ref[:, n * LANES : (n + 2) * LANES] = lax.dot_general(
             q, k, (((1,), (1,)), ((), ())), preferred_element_type=F32
         )
 
 
-def weigh(s_ref, w_ref, m_ref, t_ref, limit):
-    rows, keys = s_ref.shape
-    lane = lax.broadcasted_iota(jnp.int32, (8, LANES), 1)
-    sub = lax.broadcasted_iota(jnp.int32, (8, LANES), 0)
-    ahead = lane - jnp.where(sub >= 4, 1, 0)
-    for v in range(rows // 8):
+def iotas():
+    return tuple(lax.broadcasted_iota(jnp.int32, (8, LANES), dim) for dim in range(2))
+
+
+def fill_bias(bias_ref, limit):
+    sub, lane = iotas()
+    key = 32 * (lane >> 1) + (lane & 1) - (sub >> 2)
+    for d in range(BIASES):
+        bias_ref[d] = jnp.where(key > limit + 2 * (d - TILES + 1), -1e30, 0.0)
+
+
+def weigh(s_ref, w_ref, m_ref, t_ref, bias_ref):
+    for v in range(s_ref.shape[0] // 8):
         at = slice(8 * v, 8 * v + 8)
-        xs = [s_ref[at, n : n + LANES] for n in range(0, keys, LANES)]
-        xs[-1] = jnp.where(ahead > limit + 2 * v, -jnp.inf, xs[-1])
+        xs = []
+        for n in range(TILES):
+            x = s_ref[at, n * LANES : n * LANES + LANES]
+            d = v - n + TILES - 1
+            xs.append(x + bias_ref[d] if d < BIASES else x)
         top = tree(jnp.maximum, xs)
         ws = [jnp.exp2((x - top) * SCALE) for x in xs]
         for n, w in enumerate(ws):
@@ -65,46 +78,99 @@
     return top * SCALE + jnp.log2(total)
 
 
-def spread(w_ref, f_ref, vert_ref, slash_ref, over_ref, group):
-    rows, keys = w_ref.shape
-    tiles = keys // LANES
-    lane = lax.broadcasted_iota(jnp.int32, (8, LANES), 1)
-    zero = jnp.zeros((8, LANES), F32)
-    vert = [zero] * tiles
-    slash = [zero] * (tiles + 1)
-    for v in range(rows // 8):
+def accumulate(w_ref, f_ref, acc_ref):
+    groups = w_ref.shape[0] // 8
+    vert = [None] * TILES
+    diag = [None] * TAUS
+    add = lambda a, b: b if a is None else a + b
+    for v in range(groups):
         at = slice(8 * v, 8 * v + 8)
-        shift = LAST - 2 - 2 * v
         factor = f_ref[at, :]
-        wrapped = lane < shift
-        before = zero
-        for n in range(tiles):
+        start = groups - 1 - v
+        for n in range(TILES):
             p = w_ref[at, n * LANES : n * LANES + LANES] * factor
-            vert[n] = vert[n] + p
-            if shift:
-                turned = pltpu.roll(p, shift, 1)
-                p = jnp.where(wrapped, before, turned)
-                before = turned
-            slash[n] = slash[n] + p
-        if shift:
-            slash[tiles] = slash[tiles] + jnp.where(wrapped, before, 0.0)
-    before = zero
-    heads = slice(4 * group, 4 * group + 4)
-    for n in range(tiles + 1):
-        turned = pltpu.roll(slash[n], 1, 1)
-        y = jnp.where(lane < 1, before, turned)[0:4] + slash[n][4:8]
-        before = turned
-        if n < tiles:
-            slash_ref[heads, n * LANES : n * LANES + LANES] = y
-            vert_ref[heads, n * LANES : n * LANES + LANES] = vert[n][0:4] + vert[n][4:8]
-        else:
-            over_ref[heads, :] = y
+            vert[n] = add(vert[n], p)
+            diag[start + n] = add(diag[start + n], p)
+        acc_ref[start + TILES - 1] = diag[start + TILES - 1]
+    for t in range(TILES - 1):
+        acc_ref[t] = diag[t]
+    for n in range(TILES):
+        acc_ref[TAUS + n] = vert[n]
+
+
+def natural(tiles):
+    _, lane = iotas()
+    turned = [tiles[0]] + [pltpu.roll(tiles[n], 8 * n, 1) for n in range(1, TILES)]
+    turned = [turned[-n] for n in range(TILES)]
+    for bit in range(4):
+        step = ((lane >> (3 + bit)) & 1) == 1
+        turned = [jnp.where(step, turned[n - (1 << bit)], turned[n]) for n in range(TILES)]
+    return [interleaved(x, 8 * n) for n, x in enumerate(turned)]
+
+
+def interleaved(x, start=0):
+    _, lane = iotas()
+    source = (start + ((lane >> 1) & 15) * 8 + (lane >> 5) * 2 + (lane & 1)) & (LANES - 1)
+    return jnp.take_along_axis(x, source, axis=1)
+
+
+def both(first, second):
+    sub, _ = iotas()
+    return jnp.where(sub < 4, first, second)
+
+
+def folded(x):
+    return x + pltpu.roll(x, 4, 0)
+
+
+def whole_lanes(acc_ref):
+    _, lane = iotas()
+    inside, outside = [], []
+    for n in range(TILES):
+        x, y = acc_ref[n], None
+        for c in range(1, 3):
+            if TILES * c + n < TAUS:
+                turned = pltpu.roll(acc_ref[TILES * c + n], 2 * c, 1)
+                x = x + jnp.where(lane >= 2 * c, turned, 0.0)
+                past = jnp.where(lane < 2 * c, turned, 0.0)
+                y = past if y is None else y + past
+        inside.append(x)
+        outside.append(y)
+    return inside, outside
+
+
+def settle(acc_refs):
+    _, lane = iotas()
+    odd = (lane & 1) == 1
+    turn = lambda x: pltpu.roll(x, 4, 0)
+    (in0, out0), (in1, out1) = (whole_lanes(acc_ref) for acc_ref in acc_refs)
+    upper = lambda xs, ys: [both(x, turn(y)) for x, y in zip(xs, ys)]
+    lower = lambda xs, ys: [both(turn(x), y) for x, y in zip(xs, ys)]
+    late, same = upper(in0, in1), lower(in0, in1)
+    last = pltpu.roll(late[-1], 1, 1)
+    overs = []
+    for past in (upper(out0, out1), lower(out0, out1)):
+        past = [past[0]] + [pltpu.roll(past[n], 8 * n, 1) for n in range(1, TILES)]
+        overs.append(interleaved(tree(jnp.add, past)))
+    over = jnp.where(lane < 1, last, pltpu.roll(overs[0], 1, 1)) + overs[1]
+
+    def ordered():
+        up = [pltpu.roll(x, 1, 1) for x in late[:-1]]
+        down = [pltpu.roll(x, LANES - 1, 1) for x in late[:-1]]
+        up.append(last)
+        moved = [jnp.where(odd, up[0], jnp.where(lane < 1, 0.0, last))]
+        moved += [jnp.where(odd, up[n], down[n - 1]) for n in range(1, TILES)]
+        slash = natural([x + y for x, y in zip(moved, same)])
+        vert = natural([both(*(folded(acc_ref[TAUS + n]) for acc_ref in acc_refs)) for n in range(TILES)])
+        return vert, slash
+
+    return over, ordered
 
 
 def kernel(
-    q_hbm, k_hbm, vert_hbm, slash_hbm,
-    qg, kv, sa, sb, wv, mv, tv, mt, fv, vo, so, over, over_in, st1, st2, total,
-    q_sem, k_sem, o_sem,
+    q_hbm, k_hbm, vo, so,
+    qv, qg, kv, sa, sb, wv, mv, tv, mt, fv, acc, bias, over, over_in, st1, st2, total,
+    q_sem, k_sem,
     z_send, z_recv, y_send, y_recv, c_send, c_recv,
     s1_send, s1_recv, s2_send, s2_recv, d_send, d_recv,
 ):
@@ -117,13 +183,24 @@
     r_peer = lambda n: z * NR + lax.rem(r + n, NR)
     ahead, behind = lax.rem(seq + 1, NZ * NR), lax.rem(seq + NZ * NR - 1, NZ * NR)
     count = lax.axis_size("seq")
-    limit = LAST + jnp.where(seq == count - 1, 0, 1000)
-
-    own = pltpu.make_async_copy(q_hbm, qg.at[z, y, c], q_sem)
+    limit = so.shape[2] - LAST + jnp.where(seq == count - 1, 0, 1 << 20)
+
+    own = pltpu.make_async_copy(q_hbm, qv, q_sem)
     own.start()
-    key_copy = lambda n: pltpu.make_async_copy(k_hbm.at[n], kv.at[n], k_sem.at[n])
-    for n in range(layers):
-        key_copy(n).start()
+
+    def key_copies(layer, carry):
+        rows = k_hbm.at[layer].reshape(8, 8, 4, 8, k_hbm.shape[2])
+        for low in range(4):
+            for m in range(8):
+                pltpu.make_async_copy(
+                    rows.at[:, m, :, pl.ds(2 * low, 2), :],
+                    kv.at[layer, low, :, :, pl.ds(2 * m, 2), :],
+                    k_sem.at[layer],
+                ).start()
+        return carry
+
+    def keys_here(layer):
+        pltpu.make_async_copy(kv.at[layer], kv.at[layer], k_sem.at[layer]).wait()
 
     barrier = pltpu.get_barrier_semaphore()
     greeted = [z_peer(n) for n in range(1, NZ)] + [r_peer(n) for n in range(1, NR)] + [ahead, behind]
@@ -183,15 +260,20 @@
     def queries(layer, group):
         return qg[:, :, :, layer, group].reshape(-1, HD)
 
+    lax.fori_loop(0, CHUNK, key_copies, 0)
     own.wait()
+    block = qv[...].astype(F32).reshape(layers, -1, HD).astype(BF16)
+    qg[z, y, c] = block.reshape(qg.shape[3:])
+    fill_bias(bias, limit)
     pl.semaphore_wait(barrier, len(greeted))
     for k in range(chunks):
         for n in range(1, NZ):
             z_copy(k, n, z).start()
+    lax.fori_loop(CHUNK, layers, key_copies, 0)
     z_to_y(0)
     z_to_y(1)
     y_to_c(0)
-    key_copy(0).wait()
+    keys_here(0)
     c_copy(0, 1 - c).wait_recv()
     score(queries(0, 0), kv, 0, 0, sa)
 
@@ -213,19 +295,19 @@
             layer = CHUNK * k + j
             following = jnp.minimum(layer + 1, layers - 1)
             score(queries(layer, 1), kv, layer, 1, sb)
-            weigh(sa, wv.at[layer, 0], mv.at[0], tv.at[0], limit)
+            weigh(sa, wv.at[layer, 0], mv.at[0], tv.at[0], bias)
             gather_stats(k, 2 * j, mv.at[0], tv.at[0], mt.at[layer, 0])
 
             @pl.when(layer + 1 < layers)
             def _():
-                key_copy(layer + 1).wait()
+                keys_here(layer + 1)
 
             @pl.when((j == CHUNK - 1) & (k + 1 < chunks))
             def _():
                 c_copy(k + 1, 1 - c).wait_recv()
 
             score(queries(following, 0), kv, following, 0, sa)
-            weigh(sb, wv.at[layer, 1], mv.at[1], tv.at[1], limit)
+            weigh(sb, wv.at[layer, 1], mv.at[1], tv.at[1], bias)
             gather_stats(k, 2 * j + 1, mv.at[1], tv.at[1], mt.at[layer, 1])
             return carry
 
@@ -240,40 +322,39 @@
         return carry
 
     lax.fori_loop(0, chunks, first_pass, 0)
-
-    def out_copies(k):
-        return [
-            pltpu.make_async_copy(vo.at[part(k)], vert_hbm.at[part(k)], o_sem.at[k, 0]),
-            pltpu.make_async_copy(so.at[part(k)], slash_hbm.at[part(k)], o_sem.at[k, 1]),
-        ]
 
     def finish(k):
         d_copy(k).wait_recv()
         for j in range(CHUNK):
             so[CHUNK * k + j, :, 0:LANES] = so[CHUNK * k + j, :, 0:LANES] + over_in[CHUNK * k + j]
-        for copy in out_copies(k):
-            copy.start()
 
     def second_pass(k, carry):
         for n in range(1, NR):
             s2_copy(k, n, lax.rem(r + NR - n, NR)).wait_recv()
         total[...] = math.log2(so.shape[2] * count / LAST) - combined([st2[k, n] for n in range(NR)])
-
-        def layer_pass(j, carry):
-            layer = CHUNK * k + j
+        for j in range(CHUNK):
             for group in range(2):
                 for half in range(2):
                     at = slice(half * LANES, half * LANES + LANES)
-                    offset = total[pl.ds(4 * j + 2 * group + half, 1), :]
-                    fv[group, at, :] = jnp.exp2(mt[layer, group, :, at] * SCALE + offset).T
-                spread(
-                    wv.at[layer, group], fv.at[group],
-                    vo.at[layer], so.at[layer], over.at[layer], group,
-                )
+                    row = 4 * j + 2 * group + half
+                    logs = mt[CHUNK * k + j, group, :, at] * SCALE + total[row : row + 1, :]
+                    fv[j, group, at, :] = jnp.exp2(logs).T
+
+        def sums(n, carry):
+            j, group = n // 2, lax.rem(n, 2)
+            accumulate(wv.at[CHUNK * k + j, group], fv.at[j, group], acc.at[j, group])
             return carry
 
-        lax.fori_loop(0, CHUNK, layer_pass, 0)
+        lax.fori_loop(0, 2 * CHUNK, sums, 0)
+        rest = []
+        for j in range(CHUNK):
+            over[CHUNK * k + j], ordered = settle([acc.at[j, 0], acc.at[j, 1]])
+            rest.append(ordered)
         d_copy(k).start()
+        for j in range(CHUNK):
+            for ref, tiles in zip((vo, so), rest[j]()):
+                for n in range(TILES):
+                    ref[CHUNK * k + j, :, n * LANES : n * LANES + LANES] = tiles[n]
 
         @pl.when(k == 0)
         def _():
@@ -298,8 +379,6 @@
             s2_copy(k, n, r).wait_send()
         c_copy(k, c).wait_send()
         d_copy(k).wait_send()
-        for copy in out_copies(k):
-            copy.wait()
         return carry
 
     lax.fori_loop(0, chunks, drain, 0)
@@ -312,26 +391,27 @@
     per_group = heads // groups
     rows = LAST * per_group
     chunks = layers // CHUNK
-    q = tail_queries.reshape(layers, groups, per_group, HD)
+    q = tail_queries.reshape(layers, heads * HD)
     out = jax.ShapeDtypeStruct((layers, heads, key_count), F32)
     dma = pltpu.SemaphoreType.DMA
     return pl.pallas_call(
         kernel,
         out_shape=(out, out),
         in_specs=[pl.BlockSpec(memory_space=pl.ANY)] * 2,
-        out_specs=[pl.BlockSpec(memory_space=pl.ANY)] * 2,
+        out_specs=[pl.BlockSpec(memory_space=pltpu.VMEM)] * 2,
         scratch_shapes=[
+            pltpu.VMEM((layers, heads * HD), BF16),
             pltpu.VMEM((NZ, NY, NC, layers, groups, per_group, HD), BF16),
-            pltpu.VMEM((layers, key_count, width), BF16),
+            pltpu.VMEM((layers, 4, 8, 4, 16, width), BF16),
             pltpu.VMEM((rows, key_count), F32),
             pltpu.VMEM((rows, key_count), F32),
             pltpu.VMEM((layers, groups, rows, key_count), F32),
             pltpu.VMEM((groups, rows, LANES), F32),
             pltpu.VMEM((groups, rows, LANES), F32),
             pltpu.VMEM((layers, groups, LANES, rows), F32),
-            pltpu.VMEM((groups, rows, LANES), F32),
-            pltpu.VMEM((layers, heads, key_count), F32),
-            pltpu.VMEM((layers, heads, key_count), F32),
+            pltpu.VMEM((CHUNK, groups, rows, LANES), F32),
+            pltpu.VMEM((CHUNK, groups, TAUS + TILES, 8, LANES), F32),
+            pltpu.VMEM((BIASES, 8, LANES), F32),
             pltpu.VMEM((layers, heads, LANES), F32),
             pltpu.VMEM((layers, heads, LANES), F32),
             pltpu.VMEM((chunks, NZ, 8, LANES), F32),
@@ -339,7 +419,6 @@
             pltpu.VMEM((8, LANES), F32),
             dma,
             dma((layers,)),
-            dma((chunks, 2)),
             dma((chunks, NZ - 1)),
             dma((chunks, NZ - 1)),
             dma((chunks, NY - 1)),
@@ -354,7 +433,7 @@
             dma((chunks,)),
         ],
         compiler_params=pltpu.CompilerParams(
-            collective_id=0, has_side_effects=True, vmem_limit_bytes=67043328
+            collective_id=0, has_side_effects=True, vmem_limit_bytes=65900000
         ),
     )(q, keys)
 

time: 66.1 us -> 60.9 us (0.921)
  Pallas kernels: 59.9 us -> 56.1 us
  local copies, waits for them, and re-layouts: 5.33 us -> 3.95 us
    pallas_call x1, Pallas kernels: 59.9 us -> 56.1 us  [on_device(): pl.pallas_call(kernel, out_shape=(out, out), in_specs=[pl.BlockSpec(memor...]
    reshape x1 -> x0, local copies, waits for them, and re-layouts: 1.38 us -> none  [on_device(): q = tail_queries.reshape(layers, groups, per_group, HD)]
where the time goes in v2:
time: 60.9 us; the launch traced here: 60.7 us
  Pallas kernels  56.1 us (92%)
  local copies, waits for them, and re-layouts  3.95 us (6%)
  between operations  0.64 us (1%)
    pallas_call x1, Pallas kernels, on_device(): pl.pallas_call(kernel, out_shape=(out, out), in_specs=[pl.BlockSpec(memor...  56.1 us
    unnamed x2, local copies, waits for them, and re-layouts  3.95 us

profile of v2, /device:TPU:1, one launch (start us, length us, event | category | flops | bytes accessed | tf_op | source)
XLA Modules:
  0.0 60.7 jit_solution(6858961743237427722)
XLA Ops:
  0.6 56.1 %shard_map.41 = (f32[10,8,2048]{2,1,0:T(8,128)}, f32[10,8,2048]{2,1,0:T(8,128)}) custom-call(bf16[10,1024]{1,0:T(8,128)(2,1)} %bitcast.1, bf16[10,2048,256]{2,1,0:T(8,128)(2,1)} %k_hbm.1), custom_call_target="tpu_custom_call" | custom-call | tf_op jit(solution)/shard_map/pallas_call | solution.py:397
  56.7 2.0 %copy.6 = f32[10,8,2048]{2,1,0:T(8,128)} copy(f32[10,8,2048]{2,1,0:T(8,128)} %get-tuple-element.4) | data formatting | bytes 1310720
  58.7 2.0 %copy.7 = f32[10,8,2048]{2,1,0:T(8,128)} copy(f32[10,8,2048]{2,1,0:T(8,128)} %get-tuple-element.5) | data formatting | bytes 1310720

commit v3 on v2

--- a/solution.py
+++ b/solution.py
@@ -216,16 +216,16 @@
     part = lambda k: pl.ds(CHUNK * k, CHUNK)
 
     def z_copy(k, n, zz):
-        block = qg.at[zz, y, c, part(k)]
+        block = qg.at[zz, y, c, k]
         return remote(block, block, z_send.at[k, n - 1], z_recv.at[k, n - 1], z_peer(n))
 
     def y_copy(k, n, yy):
-        block = qg.at[:, yy, c, part(k)]
+        block = qg.at[:, yy, c, k]
         peer = z * NR + lax.rem(y + n, NY) * NC + c
         return remote(block, block, y_send.at[k, n - 1], y_recv.at[k, n - 1], peer)
 
     def c_copy(k, cc):
-        block = qg.at[:, :, cc, part(k)]
+        block = qg.at[:, :, cc, k]
         return remote(block, block, c_send.at[k], c_recv.at[k], z * NR + y * NC + 1 - c)
 
     def s1_copy(k, n, zz):
@@ -266,13 +266,21 @@
     qg[z, y, c] = block.reshape(qg.shape[3:])
     fill_bias(bias, limit)
     pl.semaphore_wait(barrier, len(greeted))
-    for k in range(chunks):
+    def z_starts(k, carry):
         for n in range(1, NZ):
             z_copy(k, n, z).start()
+        return carry
+
+    lax.fori_loop(0, layers, z_starts, 0)
     lax.fori_loop(CHUNK, layers, key_copies, 0)
-    z_to_y(0)
-    z_to_y(1)
+
+    def z_passes(k, carry):
+        z_to_y(k)
+        return carry
+
+    lax.fori_loop(0, layers, z_passes, 0)
     y_to_c(0)
+    y_to_c(1)
     keys_here(0)
     c_copy(0, 1 - c).wait_recv()
     score(queries(0, 0), kv, 0, 0, sa)
@@ -283,14 +291,6 @@
             st1[k, z, pl.ds(2 * row + half, 1), :] = found[:, half * LANES : half * LANES + LANES]
 
     def first_pass(k, carry):
-        @pl.when(k + 1 < chunks)
-        def _():
-            y_to_c(k + 1)
-
-        @pl.when(k + 2 < chunks)
-        def _():
-            z_to_y(k + 2)
-
         def layer_pass(j, carry):
             layer = CHUNK * k + j
             following = jnp.minimum(layer + 1, layers - 1)
@@ -298,13 +298,14 @@
             weigh(sa, wv.at[layer, 0], mv.at[0], tv.at[0], bias)
             gather_stats(k, 2 * j, mv.at[0], tv.at[0], mt.at[layer, 0])
 
+            @pl.when(layer + 2 < layers)
+            def _():
+                y_to_c(layer + 2)
+
             @pl.when(layer + 1 < layers)
             def _():
                 keys_here(layer + 1)
-
-            @pl.when((j == CHUNK - 1) & (k + 1 < chunks))
-            def _():
-                c_copy(k + 1, 1 - c).wait_recv()
+                c_copy(layer + 1, 1 - c).wait_recv()
 
             score(queries(following, 0), kv, following, 0, sa)
             weigh(sb, wv.at[layer, 1], mv.at[1], tv.at[1], bias)
@@ -315,9 +316,9 @@
         for n in range(1, NZ):
             s1_copy(k, n, z).start()
 
-        @pl.when(k > 0)
+        @pl.when(k > 1)
         def _():
-            s1_to_s2(k - 1)
+            s1_to_s2(k - 2)
 
         return carry
 
@@ -356,32 +357,38 @@
                 for n in range(TILES):
                     ref[CHUNK * k + j, :, n * LANES : n * LANES + LANES] = tiles[n]
 
-        @pl.when(k == 0)
+        @pl.when(k < 2)
         def _():
-            s1_to_s2(chunks - 1)
-
-        @pl.when(k > 0)
+            s1_to_s2(chunks - 2 + k)
+
+        @pl.when(k > 1)
         def _():
-            finish(k - 1)
+            finish(k - 2)
 
         return carry
 
     lax.fori_loop(0, chunks, second_pass, 0)
+    finish(chunks - 2)
     finish(chunks - 1)
 
     def drain(k, carry):
         for n in range(1, NZ):
             z_copy(k, n, z).wait_send()
-            s1_copy(k, n, z).wait_send()
         for n in range(1, NY):
             y_copy(k, n, y).wait_send()
+        c_copy(k, c).wait_send()
+        return carry
+
+    def drain_stats(k, carry):
+        for n in range(1, NZ):
+            s1_copy(k, n, z).wait_send()
         for n in range(1, NR):
             s2_copy(k, n, r).wait_send()
-        c_copy(k, c).wait_send()
         d_copy(k).wait_send()
         return carry
 
-    lax.fori_loop(0, chunks, drain, 0)
+    lax.fori_loop(0, layers, drain, 0)
+    lax.fori_loop(0, chunks, drain_stats, 0)
 
 
 def on_device(tail_queries, keys):
@@ -392,7 +399,7 @@
     rows = LAST * per_group
     chunks = layers // CHUNK
     q = tail_queries.reshape(layers, heads * HD)
-    out = jax.ShapeDtypeStruct((layers, heads, key_count), F32)
+    out = pltpu.VMEM((layers, heads, key_count), F32)
     dma = pltpu.SemaphoreType.DMA
     return pl.pallas_call(
         kernel,
@@ -419,12 +426,12 @@
             pltpu.VMEM((8, LANES), F32),
             dma,
             dma((layers,)),
-            dma((chunks, NZ - 1)),
-            dma((chunks, NZ - 1)),
-            dma((chunks, NY - 1)),
-            dma((chunks, NY - 1)),
-            dma((chunks,)),
-            dma((chunks,)),
+            dma((layers, NZ - 1)),
+            dma((layers, NZ - 1)),
+            dma((layers, NY - 1)),
+            dma((layers, NY - 1)),
+            dma((layers,)),
+            dma((layers,)),
             dma((chunks, NZ - 1)),
             dma((chunks, NZ - 1)),
             dma((chunks, NR - 1)),
@@ -433,7 +440,7 @@
             dma((chunks,)),
         ],
         compiler_params=pltpu.CompilerParams(
-            collective_id=0, has_side_effects=True, vmem_limit_bytes=65900000
+            collective_id=0, has_side_effects=True, vmem_limit_bytes=64600000
         ),
     )(q, keys)
 

time: 60.9 us -> 54.1 us (0.89)
  Pallas kernels: 56.1 us -> 51 us
  local copies, waits for them, and re-layouts: 3.95 us -> 1.67 us
    pallas_call x1, Pallas kernels: 56.1 us -> 51 us  [on_device(): pl.pallas_call(kernel, out_shape=(out, out), in_specs=[pl.BlockSpec(memor...]
    unnamed x2, local copies, waits for them, and re-layouts: 3.95 us -> 1.67 us
where the time goes in v3:
time: 54.1 us; the launch traced here: 53.3 us
  Pallas kernels  51 us (94%)
  local copies, waits for them, and re-layouts  1.67 us (3%)
  between operations  0.64 us (1%)
    pallas_call x1, Pallas kernels, on_device(): pl.pallas_call(kernel, out_shape=(out, out), in_specs=[pl.BlockSpec(memor...  51 us
    unnamed x2, local copies, waits for them, and re-layouts  1.67 us

profile of v3, /device:TPU:1, one launch (start us, length us, event | category | flops | bytes accessed | tf_op | source)
XLA Modules:
  0.0 53.3 jit_solution(5886472084190581808)
XLA Ops:
  0.6 51.0 %shard_map.41 = (f32[10,8,2048]{2,1,0:T(8,128)S(1)}, f32[10,8,2048]{2,1,0:T(8,128)S(1)}) custom-call(bf16[10,1024]{1,0:T(8,128)(2,1)} %bitcast.1, bf16[10,2048,256]{2,1,0:T(8,128)(2,1)} %k_hbm.1), custom_call_target="tpu_custom_call" | custom-call | tf_op jit(solution)/shard_map/pallas_call | solution.py:404
  51.6 0.8 %copy.6 = f32[10,8,2048]{2,1,0:T(8,128)} copy(f32[10,8,2048]{2,1,0:T(8,128)S(1)} %get-tuple-element.2) | data formatting | bytes 1310720
  52.5 0.8 %copy.7 = f32[10,8,2048]{2,1,0:T(8,128)} copy(f32[10,8,2048]{2,1,0:T(8,128)S(1)} %get-tuple-element.3) | data formatting | bytes 1310720
